TPU v7x, 8 devices: a whole 2x2x1 slice. The times are simulated.
8 devices in a mesh: model: 2 (over z, y), data: 2 (over x), stage: 2 (over core).
Axes of the slice: x: 2, y: 2, z: 1, core: 2. Of those that a mesh axis runs over, the one named last changes fastest.
Arguments:
- w_up: float32 [2, 1280, 5120], P('stage', None, 'model')
- w_down: float32 [2, 5120, 1280], P('stage', 'model')
- m_up: float32 [2, 1280, 5120], P('stage', None, 'model')
- m_down: float32 [2, 5120, 1280], P('stage', 'model')
- v_up: float32 [2, 1280, 5120], P('stage', None, 'model')
- v_down: float32 [2, 5120, 1280], P('stage', 'model')
- g_up: float32 [2, 2, 1280, 5120], P('data', 'stage', None, 'model')
- g_down: float32 [2, 2, 5120, 1280], P('data', 'stage', 'model')
- acts_last: bfloat16 [2, 512, 1280], P('stage', 'data')
- grad_out: bfloat16 [512, 1280], P('data')
- x_next: bfloat16 [3, 512, 1280], P(None, 'data')
- learn_rate: float32 [1], replicated
- max_norm: float32 [1], replicated
Outputs:
- output 1: float32 [2, 1280, 5120], P('stage', None, 'model')
- output 2: float32 [2, 5120, 1280], P('stage', 'model')
- output 3: float32 [2, 1280, 5120], P('stage', None, 'model')
- output 4: float32 [2, 5120, 1280], P('stage', 'model')
- output 5: float32 [2, 1280, 5120], P('stage', None, 'model')
- output 6: float32 [2, 5120, 1280], P('stage', 'model')
- output 7: bfloat16 [3, 512, 1280], P(None, 'data')
All inputs are finite; a program needn't handle non-finite values.
Results may differ from a plain program's by a relative error of at most 0.00703998.
Values are sent between devices in bfloat16 or wider.
A program may use at most 1 GiB of HBM per device.

v0:
```python
import functools

import jax
import jax.numpy as jnp
from jax import lax
from jax.experimental import pallas as pl
from jax.experimental.pallas import tpu as pltpu
from jax.sharding import PartitionSpec as P


ADAM_STEP = 10
BETA_ONE = 0.9
BETA_TWO = 0.95
ADAM_EPS = 1e-8
WEIGHT_DECAY = 0.1
NORM_EPS = 1e-6
ONE_CORR = 1.0 - BETA_ONE ** ADAM_STEP
TWO_CORR = 1.0 - BETA_TWO ** ADAM_STEP
ROOT_EPS = ADAM_EPS * TWO_CORR ** 0.5
ROOT_GAIN = TWO_CORR ** 0.5 / ONE_CORR
TINY = 1.1754944e-38
HUGE = 3.4028235e38
GELU_A = 0.7978845608028654
GELU_B = 0.044715
NT = (((1,), (1,)), ((), ()))
TN = (((0,), (0,)), ((), ()))
MESH = pl.DeviceIdType.MESH
VMEM_MAX = 67_043_328
CHUNK = 128
SLOTS = 11
AHEAD = 7
SPARE = 5 << 19
F32 = jnp.float32
BF16 = jnp.bfloat16


def gelu_parts(z):
    t = jnp.tanh(GELU_A * (z + GELU_B * (z * z * z)))
    return t, z * (0.5 * (1.0 + t))


def gelu_slope(z, t):
    return 0.5 * (1.0 + t) + 0.5 * z * (1.0 - t * t) * (GELU_A * (1.0 + 3.0 * GELU_B * z * z))


def dot(a, b, dims=(((1,), (0,)), ((), ()))):
    return lax.dot_general(a, b, dims, preferred_element_type=F32)


def positions():
    return lax.axis_index("model"), lax.axis_index("data"), lax.axis_index("stage")


def entry_barrier(peers):
    barrier = pltpu.get_barrier_semaphore()
    for peer in peers:
        pl.semaphore_signal(barrier, inc=1, device_id=peer, device_id_type=MESH)
    pl.semaphore_wait(barrier, len(peers))


def remote(src, dst, send, recv, peer):
    return pltpu.make_async_remote_copy(src_ref=src, dst_ref=dst, send_sem=send, recv_sem=recv, device_id=peer, device_id_type=MESH)


def adamw(scale, rate, w, mom, sec, mean):
    grad = scale * mean
    mom_new = BETA_ONE * mom + (1.0 - BETA_ONE) * grad
    sec_new = BETA_TWO * sec + ((1.0 - BETA_TWO) * grad) * grad
    root = sec_new * lax.rsqrt(jnp.minimum(sec_new + TINY, HUGE))
    w_new = w * (1.0 - rate * WEIGHT_DECAY) - (rate * ROOT_GAIN) * (mom_new / (root + ROOT_EPS))
    return w_new, mom_new, sec_new


def grad_kernel(n_chunk, width, w1, w2, g1, g2, m1, v1, m2, v2, acts, dy, x, max_norm, rate,
                gr1, gr2, gs1, clip, act_half,
                gs2, w1b, w2b, part, got, x_buf, sq1, sq2, sq_out, sq_in,
                w_sem, g_sem, send1, send2, recv1, recv2, part_sem, gvec_sem, sq_send, sq_recv,
                row_sem, act_sem, f_sem, rs_send, rs_recv, out_sem):
    m, d, s = positions()
    peer_x = (m, 1 - d, s)
    peer_y = (1 - m, d, s)
    peer_c = (m, d, 1 - s)
    peer_d = (1 - m, d, 1 - s)
    d_model = w1.shape[0]
    is_last = s == 1
    is_first = s == 0

    def loads(j):
        slot = lax.rem(j, 2)
        cols = pl.ds(pl.multiple_of(j * width, width), width)
        return (pltpu.make_async_copy(w1.at[:, cols], w1b.at[slot], w_sem.at[0, slot]),
                pltpu.make_async_copy(w2.at[cols, :], w2b.at[slot], w_sem.at[1, slot]),
                pltpu.make_async_copy(g2.at[cols, :], gs2.at[j], g_sem.at[0, slot]),
                pltpu.make_async_copy(g1.at[:, cols], gs1.at[j], g_sem.at[1, slot]))

    acts_buf, gvec = x_buf.at[2:4], x_buf.at[4:6]
    load_acts = pltpu.make_async_copy(acts, acts_buf, act_sem)
    load_dy = pltpu.make_async_copy(dy, gvec, row_sem)
    load_x = pltpu.make_async_copy(x, x_buf, row_sem)

    load_acts.start()

    @pl.when(is_last)
    def _():
        load_dy.start()

    for copy in loads(0):
        copy.start()
    entry_barrier((peer_x, peer_y, peer_c, peer_d))
    for copy in loads(1):
        copy.start()

    hand_over = remote(x_buf.at[:2], gvec, gvec_sem.at[0], gvec_sem.at[1], peer_c)
    swap_part = remote(part, got.at[:2], part_sem.at[0], part_sem.at[1], peer_y)

    @pl.when(is_last)
    def _():
        part[...] = jnp.zeros_like(part)
        load_dy.wait()

    @pl.when(is_first)
    def _():
        hand_over.wait_recv()

    load_acts.wait()

    def send_two(j):
        return remote(gs2.at[j], gr2.at[j], send2.at[j], recv2.at[j], peer_x)

    def send_one(j):
        return remote(gs1.at[j], gr1.at[j], send1.at[j], recv1.at[j], peer_x)

    @pl.loop(0, n_chunk)
    def _(j):
        slot = lax.rem(j, 2)
        copies = loads(j)
        copies[0].wait()
        up = w1b[slot].astype(BF16)
        rows = acts_buf[...].reshape(-1, d_model)
        grad = gvec[...].reshape(-1, d_model)
        z = dot(rows, up)
        t, act = gelu_parts(z)
        hid = act.astype(BF16)
        copies[2].wait()
        gs2[j] += dot(hid, grad, TN)
        send_two(j).start()
        copies[1].wait()
        grad_hid = dot(grad, w2b[slot].astype(BF16), NT)
        grad_pre = (gelu_slope(z, t) * grad_hid).astype(BF16)
        copies[3].wait()
        gs1[j] += dot(rows, grad_pre, TN)
        send_one(j).start()

        @pl.when(is_last)
        def _():
            part[...] += dot(grad_pre, up, NT).reshape(part.shape)

        @pl.when(j + 2 < n_chunk)
        def _():
            for copy in loads(j + 2):
                copy.start()

    @pl.when(is_last)
    def _():
        swap_part.start()
        swap_part.wait()
        x_buf[:2] = (gvec[...].astype(F32) + (part[...] + got[:2])).astype(BF16)
        hand_over.start()

    @pl.when(is_first)
    def _():
        load_x.start()

    n_up = n_chunk // 2
    n_pair = 2 * n_up

    def fetch(p):
        base = lax.rem(p, 3) * 6

        @pl.when(p < n_up)
        def _():
            for q, ref in enumerate((w1, m1, v1)):
                for h in (0, 1):
                    cols = pl.ds(pl.multiple_of((2 * p + h) * width, width), width)
                    pltpu.make_async_copy(ref.at[:, cols], gs1.at[base + 2 * q + h], f_sem.at[base + 2 * q + h]).start()

        @pl.when(p >= n_up)
        def _():
            cols = pl.ds(pl.multiple_of((p - n_up) * width, width), width)
            for q, ref in enumerate((w2, m2, v2)):
                for h in (0, 1):
                    rows = pl.ds(h * d_model, d_model)
                    pltpu.make_async_copy(ref.at[rows, cols], gs1.at[base + 2 * q + h], f_sem.at[base + 2 * q + h]).start()

    def arrive(p):
        base = lax.rem(p, 3) * 6
        for i in range(6):
            pltpu.make_async_copy(w1.at[:, :width], gs1.at[base + i], f_sem.at[base + i]).wait()

    def free_and_fetch(lo, hi, p):
        for i in range(lo, hi):
            send_one(i).wait_send()

        fetch(p)

    sq1[...] = jnp.zeros_like(sq1)
    sq2[...] = jnp.zeros_like(sq2)

    @pl.loop(0, n_chunk)
    def _(j):
        send_two(j).wait_recv()
        mean = (gs2[j] + gr2[j]) * 0.5
        gr2[j] = mean
        sq2[...] += jnp.sum((mean * mean).reshape(-1, 8, mean.shape[1]), axis=0)
        send_one(j).wait_recv()
        mean = (gs1[j] + gr1[j]) * 0.5
        gr1[j] = mean
        sq1[...] += jnp.sum((mean * mean).reshape(-1, 8, mean.shape[1]), axis=0)

        @pl.when(j == 10)
        def _():
            free_and_fetch(0, 6, 18 * s)

        @pl.when(j == 15)
        def _():
            free_and_fetch(6, 12, 1 + 18 * s)

    sq_out[...] = jnp.full(sq_out.shape, jnp.sum(sq1[...]) + jnp.sum(sq2[...]), F32)
    mine = 2 * m + s
    others = ((peer_y, 2 * (1 - m) + s), (peer_c, 2 * m + 1 - s), (peer_d, 2 * (1 - m) + 1 - s))
    shares = [remote(sq_out, sq_in.at[mine], sq_send.at[k], sq_recv.at[mine], peer) for k, (peer, _) in enumerate(others)]
    for copy in shares:
        copy.start()
    free_and_fetch(12, n_chunk, 2 + 15 * s)
    sq_in[mine] = sq_out[...]
    for peer, index in others:
        remote(sq_out, sq_in.at[index], sq_send.at[0], sq_recv.at[index], peer).wait_recv()
    total = (sq_in[0] + sq_in[1]) + (sq_in[2] + sq_in[3])
    clip[...] = jnp.minimum(1.0, max_norm[0] / (jnp.sqrt(total) + NORM_EPS))

    for j in range(n_chunk):
        send_two(j).wait_send()
    for copy in shares:
        copy.wait_send()

    @pl.when(is_last)
    def _():
        hand_over.wait_send()
        for p in (18, 19, 17):
            arrive(jnp.int32(p))

    @pl.when(is_first)
    def _():
        scale = clip[0, 0]
        step_rate = rate[0]
        group, half = x_buf.shape[:2]
        n_micro = group // 2
        wide = 2 * width
        n_block = d_model // width

        def new_weights(p, means):
            base = lax.rem(p, 3) * 6
            return [adamw(scale, step_rate, gs1[base + h], gs1[base + 2 + h], gs1[base + 4 + h], means[h])[0].astype(BF16) for h in (0, 1)]

        def up_pair(p):
            new = jnp.concatenate(new_weights(p, [gr1[2 * p], gr1[2 * p + 1]]), axis=1)
            act = gelu_parts(dot(x_buf[...].reshape(-1, d_model), new))[1].astype(BF16).astype(F32)
            cols = pl.ds(pl.multiple_of(lax.rem(p, n_up // 2) * wide, wide), wide)
            gs2[pl.ds((p // (n_up // 2)) * group, group), :, cols] = act.reshape(group, half, wide)

        def block(c):
            return pl.ds(pl.multiple_of(c * width, width), width)

        def down_pair(c):
            new = new_weights(n_up + c, [gr2[h * n_up:(h + 1) * n_up, :, block(c)].reshape(d_model, width) for h in (0, 1)])
            low, high = [dot(gs2[h * group:(h + 1) * group].reshape(-1, d_model).astype(BF16), new[h]) for h in (0, 1)]
            res = (low + high).reshape(group, half, width)
            for g in range(group):
                other = m if g % 2 == 0 else 1 - m
                gs2[2 * group + g // 2 + n_micro * other, :, block(c)] = res[g]
            block_copy(c).start()

        def block_copy(c):
            return remote(gs2.at[2 * group + n_micro:2 * group + 2 * n_micro, :, block(c)], got.at[:, :, block(c)], rs_send.at[c], rs_recv.at[c], peer_y)

        def ahead(p):
            @pl.when(p < n_pair)
            def _():
                fetch(p)

        load_x.wait()

        @pl.loop(0, n_up)
        def _(p):
            arrive(p)
            up_pair(p)
            ahead(p + 3)

        @pl.loop(0, n_block)
        def _(c):
            arrive(n_up + c)
            down_pair(c)
            ahead(n_up + c + 3)

        def store(c):
            return pltpu.make_async_copy(x_buf.at[:n_micro, :, block(c)], act_half.at[:, :, block(c)], out_sem.at[c])

        @pl.loop(0, n_block)
        def _(c):
            block_copy(c).wait_recv()
            for k in range(n_micro):
                rows = x_buf[2 * k + m, :, block(c)].astype(F32)
                x_buf[k, :, block(c)] = (rows + (gs2[2 * group + k, :, block(c)] + got[k, :, block(c)])).astype(BF16)
            store(c).start()

        @pl.loop(0, n_block)
        def _(c):
            block_copy(c).wait_send()
            store(c).wait()


def update_kernel(clip, rate, w1, m1, v1, gb1, w2, m2, v2, gb2, held, nw1, nm1, nv1, nw2, nm2, nv2, keep1, keep2, held_out,
                  ring, in_sem, out_sem, held_sem):
    _, deep, wide = gb1.shape
    n_slot, tall, span = ring.shape[1:]
    block = deep // tall
    per_row = w1.shape[2] // span
    n_up = per_row * (deep // tall)
    n_down = w2.shape[1] // tall
    last = n_up + n_down
    scale = clip[0, 0]
    step_rate = rate[0]
    n_held = 3
    first_held = span // wide - n_held
    kinds = ((0, n_up, span), (n_up, last, first_held * wide))

    def copies(i, kind, fetch):
        slot = lax.rem(i, n_slot)
        sem = in_sem if fetch else out_sem
        cols = kinds[kind][2]
        if kind == 0:
            refs = (w1, m1, v1) if fetch else (nw1, nm1, nv1)
            where = (0, pl.ds(pl.multiple_of(i // per_row * tall, tall), tall), pl.ds(pl.multiple_of(lax.rem(i, per_row) * span, span), span))
        else:
            refs = (w2, m2, v2) if fetch else (nw2, nm2, nv2)
            where = (0, pl.ds(pl.multiple_of((i - n_up) * tall, tall), tall), slice(0, cols))
        out = []
        for k, ref in enumerate(refs):
            pair = (ref.at[where], ring.at[k, slot, :, :cols])
            out.append(pltpu.make_async_copy(*(pair if fetch else pair[::-1]), sem.at[k, slot]))
        return out

    def each(i, act):
        if isinstance(i, int):
            kind = [n for n, (lo, hi, _) in enumerate(kinds) if lo <= i < hi][0]
            act(jnp.int32(i), kind)
            return
        for kind, (lo, hi, _) in enumerate(kinds):
            @pl.when((i >= lo) & (i < hi))
            def _():
                act(i, kind)

    def start(i, fetch):
        def act(i, kind):
            for copy in copies(i, kind, fetch):
                copy.start()

        each(i, act)

    def finish(i, fetch):
        def act(i, kind):
            for copy in copies(i, kind, fetch):
                copy.wait()

        each(i, act)

    for i in range(AHEAD):
        start(i, True)

    near = [(spot, h) for spot in range(n_held) for h in (0, 1)]

    def held_copies(spot, h):
        col = first_held + (spot + 1) % n_held
        rows, cols = slice(h * deep, (h + 1) * deep), slice(col * wide, (col + 1) * wide)
        return cols, [pltpu.make_async_copy(held_out.at[6 * spot + 2 * k + h], ref.at[0, rows, cols], held_sem.at[6 * spot + 2 * k + h])
                      for k, ref in enumerate((nw2, nm2, nv2))]

    for spot, h in near:
        cols, moves = held_copies(spot, h)
        rows = slice(h * block, (h + 1) * block)
        base = 6 * spot + h
        new, mom, sec = adamw(scale, step_rate, held[base], held[base + 2], held[base + 4], gb2[rows, :, cols].reshape(deep, wide))
        held_out[base] = new
        held_out[base + 2] = mom
        held_out[base + 4] = sec
        keep2[rows, :, cols] = new.reshape(block, -1, wide)
        for copy in moves:
            copy.start()

    def step(slot, cols, mean):
        new, mom, sec = adamw(scale, step_rate, ring[0, slot, :, cols], ring[1, slot, :, cols], ring[2, slot, :, cols], mean)
        ring[0, slot, :, cols] = new
        ring[1, slot, :, cols] = mom
        ring[2, slot, :, cols] = sec
        return new

    def compute(i, kind):
        slot = lax.rem(i, n_slot)
        if kind == 0:
            rows = pl.ds(pl.multiple_of(i // per_row * tall, tall), tall)
            for t in range(span // wide):
                col = lax.rem(i, per_row) * (span // wide) + t
                keep1[col, rows] = step(slot, slice(t * wide, (t + 1) * wide), gb1[col, rows])
        else:
            cols = slice(0, kinds[kind][2])
            keep2[i - n_up, :, cols] = step(slot, cols, gb2[i - n_up, :, cols])

    @pl.loop(0, last)
    def _(i):
        finish(i, True)
        each(i, compute)
        start(i, False)

        @pl.when(i + AHEAD < last)
        def _():
            @pl.when(i + AHEAD - n_slot >= 0)
            def _():
                finish(i + AHEAD - n_slot, False)

            start(i + AHEAD, True)

    for i in range(last - n_slot, last):
        finish(i, False)
    for spot, h in near:
        for copy in held_copies(spot, h)[1]:
            copy.wait()


def forward_kernel(from_core, from_diag, new1, new2, y,
                   hid, act, own_half, peer_half, part, part_in,
                   in_sem, p_send, p_recv, y_send, y_recv, g_send, g_recv, f_send, f_recv, ready):
    m, d, s = positions()
    n_micro, half, d_model = own_half.shape
    width = 2 * new1.shape[2]
    n_chunk, n_block = new1.shape[0] // 2, d_model // width
    peer_y = (1 - m, d, s)
    peer_c = (m, d, 1 - s)
    barrier = pltpu.get_barrier_semaphore()
    mine = pl.ds(pl.multiple_of(m * half, half), half)
    theirs = pl.ds(pl.multiple_of((1 - m) * half, half), half)
    rows_in = (pltpu.make_async_copy(from_core, act.at[:, mine, :], in_sem.at[0]),
               pltpu.make_async_copy(from_diag, act.at[:, theirs, :], in_sem.at[1]))

    @pl.when(s == 1)
    def _():
        for copy in rows_in:
            copy.start()
        pl.semaphore_signal(barrier, inc=1, device_id=peer_y, device_id_type=MESH)
        pl.semaphore_signal(barrier, inc=1, device_id=peer_c, device_id_type=MESH)

    pl.semaphore_wait(barrier, 1)

    @pl.when(s == 0)
    def _():
        pl.semaphore_signal(ready, inc=1, device_id=peer_c, device_id_type=MESH)

    def span(c):
        return pl.ds(pl.multiple_of(c * width, width), width)

    def send_part(k, c):
        return remote(part.at[k, theirs, span(c)], part_in.at[k, :, span(c)], p_send.at[k, c], p_recv.at[k, c], peer_y)

    def swap_y(k, c):
        return remote(own_half.at[k, :, span(c)], peer_half.at[k, :, span(c)], y_send.at[k, c], y_recv.at[k, c], peer_y)

    def give_own(k):
        return remote(own_half.at[k], y.at[k, mine, :], g_send.at[k], g_recv.at[k], peer_c)

    def pass_on(k):
        return remote(peer_half.at[k], y.at[k, theirs, :], f_send.at[k], f_recv.at[k], peer_c)

    @pl.when(s == 0)
    def _():
        for k in range(n_micro):
            give_own(k).wait_recv()
            pass_on(k).wait_recv()

    @pl.when(s == 1)
    def _():
        for copy in rows_in:
            copy.wait()

        for k in range(n_micro):
            @pl.loop(0, n_chunk)
            def _(j):
                up = jnp.concatenate([new1[2 * j].astype(BF16), new1[2 * j + 1].astype(BF16)], axis=1)
                hid[:, span(j)] = gelu_parts(dot(act[k], up))[1].astype(BF16)

            @pl.loop(0, n_block)
            def _(c):
                down = new2[:, :, span(c)].reshape(-1, width).astype(BF16)
                part[k, :, span(c)] = dot(hid[...], down)
                send_part(k, c).start()

        for k in range(n_micro):
            @pl.loop(0, n_block)
            def _(c):
                send_part(k, c).wait_recv()
                out = act[k, mine, span(c)].astype(F32) + (part[k, mine, span(c)] + part_in[k, :, span(c)])
                own_half[k, :, span(c)] = out.astype(BF16)
                swap_y(k, c).start()

            y[k, mine, :] = own_half[k]

        pl.semaphore_wait(ready, 1)
        for k in range(n_micro):
            give_own(k).start()
        for k in range(n_micro):
            @pl.loop(0, n_block)
            def _(c):
                swap_y(k, c).wait_recv()

            pass_on(k).start()
            y[k, theirs, :] = peer_half[k]
        for k in range(n_micro):
            @pl.loop(0, n_block)
            def _(c):
                send_part(k, c).wait_send()
                swap_y(k, c).wait_send()

            give_own(k).wait_send()
            pass_on(k).wait_send()


def solution(mesh):
    up_spec = P('stage', None, 'model')
    down_spec = P('stage', 'model', None)
    row_spec = P(None, 'data', None)
    in_specs = (up_spec, down_spec, up_spec, down_spec, up_spec, down_spec, P('data', 'stage', None, 'model'), P('data', 'stage', 'model', None), P('stage', 'data', None), P('data', None), row_spec, P(None), P(None))
    out_specs = (up_spec, down_spec, up_spec, down_spec, up_spec, down_spec, row_spec)

    def device_step(w_up, w_down, m_up, m_down, v_up, v_down, g_up, g_down, acts_last, grad_out, x_next, learn_rate, max_norm):
        d_model, ff = w_up.shape[1:]
        rows = grad_out.shape[0]
        n_micro = x_next.shape[0]
        width = CHUNK
        n_chunk = ff // width
        half = rows // 2
        hbm = pl.BlockSpec(memory_space=pl.ANY)
        vmem = pl.BlockSpec(memory_space=pltpu.VMEM)
        smem = pl.BlockSpec(memory_space=pltpu.SMEM)
        dma = pltpu.SemaphoreType.DMA
        resident = 4 * 3 * d_model * ff
        n_block = d_model // (2 * width)

        mean_up, mean_down, held, clip, act_half = pl.pallas_call(
            functools.partial(grad_kernel, n_chunk, width),
            out_shape=(pltpu.VMEM((n_chunk, d_model, width), F32),
                       pltpu.VMEM((n_chunk, width, d_model), F32),
                       pltpu.VMEM((n_chunk, d_model, width), F32),
                       jax.ShapeDtypeStruct((8, 128), F32),
                       jax.ShapeDtypeStruct((n_micro, half, d_model), BF16)),
            in_specs=[hbm] * 11 + [smem, smem],
            out_specs=(vmem, vmem, vmem, vmem, hbm),
            scratch_shapes=[
                pltpu.VMEM((n_chunk, width, d_model), F32),
                pltpu.VMEM((2, d_model, width), F32),
                pltpu.VMEM((2, width, d_model), F32),
                pltpu.VMEM((2, half, d_model), F32),
                pltpu.VMEM((n_micro, half, d_model), F32),
                pltpu.VMEM((2 * n_micro, half, d_model), BF16),
                pltpu.VMEM((8, width), F32),
                pltpu.VMEM((8, d_model), F32),
                pltpu.VMEM((8, 128), F32),
                pltpu.VMEM((4, 8, 128), F32),
                dma((2, 2)), dma((2, 2)),
                dma((n_chunk,)), dma((n_chunk,)), dma((n_chunk,)), dma((n_chunk,)),
                dma((2,)), dma((2,)), dma((3,)), dma((4,)),
                dma(()), dma(()), dma((18,)), dma((2 * n_block,)), dma((2 * n_block,)), dma((2 * n_block,)),
            ],
            compiler_params=pltpu.CompilerParams(collective_id=0, has_side_effects=True, vmem_limit_bytes=VMEM_MAX - resident - SPARE),
            name="grad_exchange",
        )(w_up[0], w_down[0], g_up[0, 0], g_down[0, 0], m_up[0], v_up[0], m_down[0], v_down[0], acts_last.reshape(2, half, d_model), grad_out.reshape(2, half, d_model), x_next.reshape(2 * n_micro, half, d_model), max_norm, learn_rate)

        from_diag = lax.ppermute(act_half, ('model', 'stage'), [(0, 3), (2, 1)])
        from_core = lax.ppermute(act_half, ('model', 'stage'), [(0, 1), (2, 3)])

        def stay(array):
            return pltpu.with_memory_space_constraint(array, pltpu.VMEM)

        up_out = jax.ShapeDtypeStruct(w_up.shape, F32)
        down_out = jax.ShapeDtypeStruct(w_down.shape, F32)
        nw1, nm1, nv1, nw2, nm2, nv2, new1, new2, _ = pl.pallas_call(
            update_kernel,
            out_shape=(up_out, up_out, up_out, down_out, down_out, down_out,
                       pltpu.VMEM(mean_up.shape, F32), pltpu.VMEM(mean_down.shape, F32), pltpu.VMEM(held.shape, F32)),
            in_specs=[smem, smem, hbm, hbm, hbm, vmem, hbm, hbm, hbm, vmem, vmem],
            out_specs=(hbm,) * 6 + (vmem, vmem, vmem),
            input_output_aliases={5: 6, 9: 7, 10: 8},
            scratch_shapes=[pltpu.VMEM((3, SLOTS, width, d_model), F32), dma((3, SLOTS)), dma((3, SLOTS)), dma((18,))],
            compiler_params=pltpu.CompilerParams(vmem_limit_bytes=VMEM_MAX - resident - SPARE),
            cost_estimate=pl.CostEstimate(flops=2000 * d_model * ff, bytes_accessed=48 * d_model * ff, transcendentals=4 * d_model * ff),
            name="update",
        )(clip, learn_rate, w_up, m_up, v_up, stay(mean_up), w_down, m_down, v_down, stay(mean_down), stay(held))

        y_next = pl.pallas_call(
            forward_kernel,
            out_shape=pltpu.VMEM(x_next.shape, BF16),
            in_specs=[hbm, hbm, vmem, vmem],
            out_specs=vmem,
            scratch_shapes=[
                pltpu.VMEM((rows, ff), BF16),
                pltpu.VMEM((n_micro, rows, d_model), BF16),
                pltpu.VMEM((n_micro, half, d_model), BF16),
                pltpu.VMEM((n_micro, half, d_model), BF16),
                pltpu.VMEM((n_micro, rows, d_model), F32),
                pltpu.VMEM((n_micro, half, d_model), F32),
                dma((2,)), dma((n_micro, n_block)), dma((n_micro, n_block)), dma((n_micro, n_block)), dma((n_micro, n_block)),
                dma((n_micro,)), dma((n_micro,)), dma((n_micro,)), dma((n_micro,)),
                pltpu.SemaphoreType.REGULAR,
            ],
            compiler_params=pltpu.CompilerParams(collective_id=1, has_side_effects=True, vmem_limit_bytes=VMEM_MAX - resident - SPARE),
            name="forward_exchange",
        )(from_core, from_diag, stay(new1), stay(new2))
        return nw1, nw2, nm1, nm2, nv1, nv2, y_next

    return jax.shard_map(device_step, mesh=mesh, in_specs=in_specs, out_specs=out_specs, check_vma=False)
```

profile of v0, /device:TPU:0, one launch (start us, length us, event | category | flops | bytes accessed | tf_op | source)
XLA Modules:
  0.0 672.8 jit_solution(18329055418277790182)
XLA Ops:
  1.9 611.7 %grad_exchange.1 = (f32[20,1280,128]{2,1,0:T(8,128)S(1)}, f32[20,128,1280]{2,1,0:T(8,128)S(1)}, f32[20,1280,128]{2,1,0:T(8,128)S(1)}, f32[8,128]{1,0:T(8,128)}, bf16[3,128,1280]{2,1,0:T(8,128)(2,1)}) custom-call(f32[1280,2560]{1,0:T(8,128)} %bitcast.11, f32[2560,1280]{1,0:T(8,128)} %bitcast.12, f32[1280,2560]{1,0:T(8,128)} %bitcast.17, ...), custom_call_target="tpu_custom_call" | custom-call | tf_op jit(solution)/shard_map/grad_exchange/pallas_call | solution.py:556
  613.7 1.4 collective-permute-start
  615.0 1.5 collective-permute-start.1
  616.6 50.2 %update.1 = (f32[1,1280,2560]{2,1,0:T(8,128)}, f32[1,1280,2560]{2,1,0:T(8,128)}, f32[1,1280,2560]{2,1,0:T(8,128)}, f32[1,2560,1280]{2,1,0:T(8,128)}, f32[1,2560,...) custom-call(f32[8,128]{1,0:T(8,128)} %get-tuple-element.20.clip, ...), custom_call_target="tpu_custom_call", output_to_operand_aliasing={{6}: (5, {}), {7}: (9, {}), {8}: (10, {})} | custom-call | flops 6553600000 | bytes 157286400 | tf_op jit(solution)/shard_map/update/pallas_call | solution.py:593
  666.8 0.0 collective-permute-done.from_core
  666.8 0.0 collective-permute-done.1.from_diag
  666.9 4.7 forward_exchange.1
  671.5 1.3 copy.27
Async XLA Ops:
  613.7 53.2 %collective-permute-start = (bf16[3,128,1280]{2,1,0:T(8,128)(2,1)}, bf16[3,128,1280]{2,1,0:T(8,128)(2,1)S(1)}, u32[]{:S(2)}, u32[]{:S(2)}) collective-permute-start(bf16[3,128,1280]{2,1,0:T(8,128)(2,1)} %get-tuple-element.30), channel_id=1, source_target_pairs={{0,1},{4,5},{2,3},{6,7}} | collective-permute-start | bytes 2949128 | tf_op jit(solution)/shard_map/ppermute | solution.py:586
  615.0 51.8 %collective-permute-start.1 = (bf16[3,128,1280]{2,1,0:T(8,128)(2,1)}, bf16[3,128,1280]{2,1,0:T(8,128)(2,1)S(1)}, u32[]{:S(2)}, u32[]{:S(2)}) collective-permute-start(bf16[3,128,1280]{2,1,0:T(8,128)(2,1)} %get-tuple-element.30), channel_id=1, source_target_pairs={{0,5},{4,1},{2,7},{6,3}} | collective-permute-start | bytes 2949128 | tf_op jit(solution)/shard_map/ppermute | solution.py:585
where the time goes:
time: 673 us
  Pallas kernels  667 us (99%)
    pallas_call x1, Pallas kernels, device_step(): pl.pallas_call(functools.partial(grad_kernel, n_chunk, width), out_shape=...  612 us
    pallas_call x1, Pallas kernels, device_step(): pl.pallas_call(update_kernel, out_shape=(up_out, up_out, up_out, down_out...  50.2 us
  transfers between devices with their start and end apart: 2, of which 0 were waited for; matrix products, arithmetic and copies ran while one was open for 0% of the time, Pallas kernels for 7%

commit v1 on v0

--- a/solution.py
+++ b/solution.py
@@ -28,7 +28,7 @@
 VMEM_MAX = 67_043_328
 CHUNK = 128
 SLOTS = 11
-AHEAD = 7
+AHEAD = 8
 SPARE = 5 << 19
 F32 = jnp.float32
 BF16 = jnp.bfloat16
@@ -99,15 +99,16 @@
     load_x = pltpu.make_async_copy(x, x_buf, row_sem)
 
     load_acts.start()
+    urgent = loads(0)
+    urgent[0].start()
 
     @pl.when(is_last)
     def _():
         load_dy.start()
 
-    for copy in loads(0):
-        copy.start()
+    urgent[2].start()
     entry_barrier((peer_x, peer_y, peer_c, peer_d))
-    for copy in loads(1):
+    for copy in (urgent[1], urgent[3], *loads(1)):
         copy.start()
 
     hand_over = remote(x_buf.at[:2], gvec, gvec_sem.at[0], gvec_sem.at[1], peer_c)

time: 673 us -> 673 us (level)
  no operation moved by 1% of the time
where the time goes in v1:
time: 673 us; the launch traced here: 672 us
  Pallas kernels  666 us (99%)
    pallas_call x1, Pallas kernels, device_step(): pl.pallas_call(functools.partial(grad_kernel, n_chunk, width), out_shape=...  612 us
    pallas_call x1, Pallas kernels, device_step(): pl.pallas_call(update_kernel, out_shape=(up_out, up_out, up_out, down_out...  49.8 us
  transfers between devices with their start and end apart: 2, of which 0 were waited for; matrix products, arithmetic and copies ran while one was open for 0% of the time, Pallas kernels for 7%

profile of v1, /device:TPU:0, one launch (start us, length us, event | category | flops | bytes accessed | tf_op | source)
XLA Modules:
  0.0 672.3 jit_solution(16146071670937403472)
XLA Ops:
  1.9 611.7 %grad_exchange.1 = (f32[20,1280,128]{2,1,0:T(8,128)S(1)}, f32[20,128,1280]{2,1,0:T(8,128)S(1)}, f32[20,1280,128]{2,1,0:T(8,128)S(1)}, f32[8,128]{1,0:T(8,128)}, bf16[3,128,1280]{2,1,0:T(8,128)(2,1)}) custom-call(f32[1280,2560]{1,0:T(8,128)} %bitcast.11, f32[2560,1280]{1,0:T(8,128)} %bitcast.12, f32[1280,2560]{1,0:T(8,128)} %bitcast.17, ...), custom_call_target="tpu_custom_call" | custom-call | tf_op jit(solution)/shard_map/grad_exchange/pallas_call | solution.py:557
  613.7 1.4 collective-permute-start
  615.0 1.5 collective-permute-start.1
  616.6 49.8 %update.1 = (f32[1,1280,2560]{2,1,0:T(8,128)}, f32[1,1280,2560]{2,1,0:T(8,128)}, f32[1,1280,2560]{2,1,0:T(8,128)}, f32[1,2560,1280]{2,1,0:T(8,128)}, f32[1,2560,...) custom-call(f32[8,128]{1,0:T(8,128)} %get-tuple-element.20.clip, ...), custom_call_target="tpu_custom_call", output_to_operand_aliasing={{6}: (5, {}), {7}: (9, {}), {8}: (10, {})} | custom-call | flops 6553600000 | bytes 157286400 | tf_op jit(solution)/shard_map/update/pallas_call | solution.py:594
  666.4 0.0 collective-permute-done.from_core
  666.4 0.0 collective-permute-done.1.from_diag
  666.4 4.7 forward_exchange.1
  671.1 1.3 copy.27
Async XLA Ops:
  613.7 52.7 %collective-permute-start = (bf16[3,128,1280]{2,1,0:T(8,128)(2,1)}, bf16[3,128,1280]{2,1,0:T(8,128)(2,1)S(1)}, u32[]{:S(2)}, u32[]{:S(2)}) collective-permute-start(bf16[3,128,1280]{2,1,0:T(8,128)(2,1)} %get-tuple-element.30), channel_id=1, source_target_pairs={{0,1},{4,5},{2,3},{6,7}} | collective-permute-start | bytes 2949128 | tf_op jit(solution)/shard_map/ppermute | solution.py:587
  615.0 51.3 %collective-permute-start.1 = (bf16[3,128,1280]{2,1,0:T(8,128)(2,1)}, bf16[3,128,1280]{2,1,0:T(8,128)(2,1)S(1)}, u32[]{:S(2)}, u32[]{:S(2)}) collective-permute-start(bf16[3,128,1280]{2,1,0:T(8,128)(2,1)} %get-tuple-element.30), channel_id=1, source_target_pairs={{0,5},{4,1},{2,7},{6,3}} | collective-permute-start | bytes 2949128 | tf_op jit(solution)/shard_map/ppermute | solution.py:586
